TPU v7x, 32 devices: a whole 2x2x4 slice. The times are simulated.
32 devices in a mesh: pair: 2 (over core), shard: 16 (over z, y, x).
Axes of the slice: x: 2, y: 2, z: 4, core: 2. Of those that a mesh axis runs over, the one named last changes fastest.
Arguments:
- master: float32 [3072, 4096], P('shard', 'pair'), may hold values from -1.5 to 1.5
- gradient: float32 [3072, 4096], P('shard', 'pair'), may hold values from -40 to 40
- first_moment: float32 [3072, 4096], P('shard', 'pair'), may hold values from -4 to 4
- second_moment: float32 [3072, 4096], P('shard', 'pair'), may hold values from 0.02 to 4
- max_norm: float32 [1], replicated, may hold values from 768 to 1536
- step_count: int32 [1], replicated, may hold values from 1 to 1000
Outputs:
- new_master: float32 [3072, 4096], P('shard', 'pair')
- new_first: float32 [3072, 4096], P('shard', 'pair')
- new_second: float32 [3072, 4096], P('shard', 'pair')
- compute_codes: bfloat16 [3072, 4096], P('pair')
- block_scales: bfloat16 [3072, 128], P('pair')
All inputs are finite; a program needn't handle non-finite values.
Results may differ from a plain program's by a relative error of at most 0.001.
The roundings to bfloat16 on the way count: a program that leaves them out, or rounds other values in their place, can miss the bound.
Values may be sent and summed in bfloat16 or wider, within the bound.
A program may use at most 192 MiB of HBM per device.

v0:
```python
import jax
import jax.numpy as jnp
from jax import lax
from jax.sharding import PartitionSpec as P

BLOCK = 32


beta_first = 0.9
beta_second = 0.99
learn_rate = 0.01
decay_rate = 0.1
adam_eps = 1e-06
scale_floor = 0.25


def quantize(weights):
    height, width = weights.shape
    blocked = weights.reshape(height, width // BLOCK, BLOCK)
    largest = jnp.max(jnp.abs(blocked), axis=2)
    scales = jnp.maximum(largest, scale_floor).astype(jnp.bfloat16)
    divided = blocked / scales.astype(jnp.float32)[:, :, None]
    return (divided.astype(jnp.bfloat16).reshape(height, width), scales)


def adam_update(master, gradient, first_moment, second_moment, max_norm, step_count, squares):
    norm_limit = max_norm[0]
    clip_factor = norm_limit / jnp.maximum(jnp.sqrt(squares), norm_limit)
    clipped = clip_factor * gradient
    new_first = beta_first * first_moment + (1.0 - beta_first) * clipped
    new_second = beta_second * second_moment + (1.0 - beta_second) * clipped * clipped
    counted = step_count[0].astype(jnp.float32)
    first_fix = 1.0 - jnp.power(jnp.full((), beta_first, jnp.float32), counted)
    second_fix = 1.0 - jnp.power(jnp.full((), beta_second, jnp.float32), counted)
    update = (
        new_first / first_fix / (jnp.sqrt(new_second / second_fix) + adam_eps) + decay_rate * master
    )
    new_master = master - learn_rate * update
    return (new_master, new_first, new_second)


def per_device(master, gradient, first_moment, second_moment, max_norm, step_count):
    squares = lax.psum(jnp.sum(gradient * gradient), ("pair", "shard"))
    new_master, new_first, new_second = adam_update(
        master, gradient, first_moment, second_moment, max_norm, step_count, squares
    )
    own_codes, own_scales = quantize(new_master)
    half_codes, half_scales = (
        lax.all_gather(own_codes, "shard", axis=0, tiled=True),
        lax.all_gather(own_scales, "shard", axis=0, tiled=True),
    )
    compute_codes, block_scales = (
        lax.all_to_all(half_codes, "pair", split_axis=0, concat_axis=1, tiled=True),
        lax.all_to_all(half_scales, "pair", split_axis=0, concat_axis=1, tiled=True),
    )
    return (new_master, new_first, new_second, compute_codes, block_scales)


def solution(mesh):
    return jax.shard_map(
        per_device,
        mesh=mesh,
        in_specs=(
            P("shard", "pair"),
            P("shard", "pair"),
            P("shard", "pair"),
            P("shard", "pair"),
            P(),
            P(),
        ),
        out_specs=(
            P("shard", "pair"),
            P("shard", "pair"),
            P("shard", "pair"),
            P("pair", None),
            P("pair", None),
        ),
        check_vma=False,
    )
```

profile of v0, /device:TPU:1, one launch (start us, length us, event | category | flops | bytes accessed | tf_op | source)
XLA Modules:
  0.0 289.1 jit_solution(9234097476753203765)
XLA Ops:
  7.2 0.0 copy-start.1
  7.2 0.0 copy-start.2
  7.2 0.0 all-gather.3.cloned.1.call-start
  7.2 3.0 %copy.36 = f32[192,2048]{0,1:T(8,128)} copy(f32[192,2048]{1,0:T(8,128)} %param.7) | data formatting | bytes 3145728 | tf_op args[1]
  10.2 0.0 copy-done.1
  10.2 1.0 multiply_reduce_fusion
  11.2 0.0 copy-done.2
  11.2 0.0 copy-start.3
  11.2 1.8 copy.39
  13.0 0.0 copy-start.4
  14.5 40.9 %psum.7 = f32[]{:T(128)} all-reduce(f32[]{:T(128)} %multiply_reduce_fusion), channel_id=1, replica_groups=mesh['pair'=2,'shard'=16] {'pair','shard'}, use_global_device_ids=true, to_apply=%region_1.0 | all-reduce | flops 1 | bytes 8 | tf_op jit(solution)/shard_map/psum | solution.py:43
  56.1 0.0 copy-done.3
  56.1 1.8 copy.37
  57.9 0.0 copy-done.4
  58.0 1.8 copy.35
  59.8 7.4 %bitcast_reduce_fusion = (bf16[192,64]{0,1:T(8,128)(2,1)S(1)}, f32[192,2048]{0,1:T(8,128)S(1)}, f32[192,2048]{0,1:T(8,128)}, f32[192,2048]{0,1:T(8,128)}) fusion(f32[192,2048]{0,1:T(8,128)} %copy.39, f32[]{:T(128)} %bitcast.2, f32[]{:T(128)} %bitcast.1, f32[192,2048]{0,1:T(8,128)} %copy.36, f32[]{:T(128)S(6)} %div.27, f32[192,2048]{0,1:T(8,128)} %copy.37, ...), kind=kLoop, calls=%fused_computation.4 | loop fusion | flops 7458816 | bytes 11034636 | tf_op jit(solution)/shard_map/reduce_max | solution.py:20
  67.2 0.2 fusion.1
  67.4 1.3 copy.40
  68.7 0.0 all-gather.3.cloned.1.call-update
  68.7 38.4 %all-gather = bf16[16,192,64]{1,2,0:T(8,128)(2,1)S(1)} all-gather(bf16[1,192,64]{1,2,0:T(8,128)(2,1)S(1)} %get-tuple-element.24), channel_id=1, replica_groups=mesh['pair'=2,'shard'=16] {'shard'}, dimensions={0}, use_global_device_ids=true | all-gather | bytes 417792 | tf_op jit(solution)/shard_map/all_gather | solution.py:50
  107.1 0.3 copy.42
  107.4 0.6 all_to_all.32
  108.0 0.8 copy.43
  108.8 12.2 %all-to-all-start.1 = ((bf16[2,1536,64]{1,2,0:T(8,128)(2,1)}), bf16[2,1536,64]{1,2,0:T(8,128)(2,1)S(1)}, u32[]{:S(2)}, u32[]{:S(2)}) async-start(bf16[2,1536,64]{1,2,0:T(8,128)(2,1)} %copy.43), calls=%async_computation.1 | async-start | bytes 786432 | tf_op jit(solution)/shard_map/all_to_all | solution.py:54
  121.0 1.7 copy.44
  122.6 0.0 copy-start
  122.6 2.9 %copy.45 = f32[192,2048]{1,0:T(8,128)} copy(f32[192,2048]{0,1:T(8,128)} %get-tuple-element.23) | data formatting | bytes 3145728
  125.5 0.0 copy-done
  125.5 1.7 copy.46
  127.2 0.0 all-to-all-done.1
  127.2 0.9 copy.48
  128.1 94.9 %all-gather.3.cloned.1.call-done = bf16[3072,2048]{1,0:T(8,128)(2,1)} async-done(((bf16[192,2048]{1,0:T(8,128)(2,1)}), bf16[3072,2048]{1,0:T(8,128)(2,1)}) %all-gather.3.cloned.1.call-update) | async-done | bytes 12582928 | tf_op jit(solution)/shard_map/all_gather | solution.py:49
  223.0 16.6 %copy.41 = bf16[2,1536,2048]{1,2,0:T(8,128)(2,1)} copy(bf16[2,1536,2048]{2,1,0:T(8,128)(2,1)} %bitcast.23) | data formatting | bytes 25165824 | tf_op jit(solution)/shard_map/all_to_all | solution.py:53
  239.6 26.0 %all_to_all.38 = bf16[2,1536,2048]{1,2,0:T(8,128)(2,1)} all-to-all(bf16[2,1536,2048]{1,2,0:T(8,128)(2,1)} %copy.41), channel_id=1, replica_groups=mesh['pair'=2,'shard'=16] {'pair'}, dimensions={0} | all-to-all | bytes 25165824 | tf_op jit(solution)/shard_map/all_to_all | solution.py:53
  265.7 16.6 %copy.47 = bf16[1536,4096]{1,0:T(8,128)(2,1)} copy(bf16[1536,4096]{0,1:T(8,128)(2,1)} %bitcast.22) | data formatting | bytes 25165824
  (1 shorter events, 0.0 us)
Async XLA Ops:
  7.2 3.0 %copy-start.1 = (f32[192,2048]{1,0:T(8,128)S(1)}, f32[192,2048]{1,0:T(8,128)}, u32[]{:S(2)}) copy-start(f32[192,2048]{1,0:T(8,128)} %param.7) | copy-start | bytes 4718596
  7.2 4.0 %copy-start.2 = (f32[192,2048]{1,0:T(8,128)S(1)}, f32[192,2048]{1,0:T(8,128)}, u32[]{:S(2)}) copy-start(f32[192,2048]{1,0:T(8,128)} %param.6) | copy-start | bytes 4718596
  7.2 215.9 %all-gather.3.cloned.1.call-start = ((), (), s32[]{:S(2)}) async-start(), calls=%async_computation.2 | async-start | bytes 13369344 | tf_op jit(solution)/shard_map/all_gather | solution.py:49
  11.2 44.9 %copy-start.3 = (f32[192,2048]{1,0:T(8,128)S(1)}, f32[192,2048]{1,0:T(8,128)}, u32[]{:S(2)}) copy-start(f32[192,2048]{1,0:T(8,128)} %param.9) | copy-start | bytes 4718596
  13.0 45.0 %copy-start.4 = (f32[192,2048]{1,0:T(8,128)S(1)}, f32[192,2048]{1,0:T(8,128)}, u32[]{:S(2)}) copy-start(f32[192,2048]{1,0:T(8,128)} %param.8) | copy-start | bytes 4718596
  108.8 18.4 %all-to-all-start.1 = ((bf16[2,1536,64]{1,2,0:T(8,128)(2,1)}), bf16[2,1536,64]{1,2,0:T(8,128)(2,1)S(1)}, u32[]{:S(2)}, u32[]{:S(2)}) async-start(bf16[2,1536,64]{1,2,0:T(8,128)(2,1)} %copy.43), calls=%async_computation.1 | async-start | bytes 786432 | tf_op jit(solution)/shard_map/all_to_all | solution.py:54
  122.6 2.9 %copy-start = (f32[192,2048]{0,1:T(8,128)S(1)}, f32[192,2048]{0,1:T(8,128)}, u32[]{:S(2)}) copy-start(f32[192,2048]{0,1:T(8,128)} %get-tuple-element.22) | copy-start | bytes 4718596
Sparse Core Ops, SparseCore 0:
  68.8 154.1 all-gather.2
where the time goes:
time: 291 us; the launch traced here: 289 us
  blocking collectives  105 us (36%)
  waiting for transfers between devices  94.9 us (33%)
  local copies, waits for them, and re-layouts  51.7 us (18%)
  between operations  16.3 us (6%)
  starting transfers between devices  12.2 us (4%)
  other arithmetic  8.64 us (3%)
    all_gather x1, waiting for transfers between devices, per_device(): lax.all_gather(own_codes, 'shard', axis=0, tiled=True)  94.9 us
    psum x1, blocking collectives, per_device(): squares = lax.psum(jnp.sum(gradient * gradient), ('pair', 'shard'))  40.9 us
    all_gather x1, blocking collectives, per_device(): lax.all_gather(own_scales, 'shard', axis=0, tiled=True)  38.4 us
    unnamed x19, local copies, waits for them, and re-layouts  32.1 us
    all_to_all x1, blocking collectives, per_device(): lax.all_to_all(half_codes, 'pair', split_axis=0, concat_axis=1, tiled=True)  26 us
    all_to_all x1, local copies, waits for them, and re-layouts, per_device(): lax.all_to_all(half_codes, 'pair', split_axis=0, concat_axis=1, tiled=True)  16.6 us
    all_to_all x1, starting transfers between devices, per_device(): lax.all_to_all(half_scales, 'pair', split_axis=0, concat_axis=1, tiled=True)  12.2 us
    reduce_max x1, other arithmetic, quantize(): largest = jnp.max(jnp.abs(blocked), axis=2)  7.41 us
  transfers between devices with their start and end apart: 2, of which 1 were waited for; matrix products, arithmetic and copies ran while one was open for 3% of the time, Pallas kernels for 0%

commit v1 on v0

v1 whole, which is shorter than its diff:
```python
import functools

import jax
import jax.numpy as jnp
from jax import lax
from jax.experimental import pallas as pl
from jax.experimental.pallas import tpu as pltpu
from jax.sharding import PartitionSpec as P

BLOCK = 32
LANES = 128

beta_first = 0.9
beta_second = 0.99
learn_rate = 0.01
decay_rate = 0.1
adam_eps = 1e-06
scale_floor = 0.25

MESH = pl.DeviceIdType.MESH
Z, Y, X = 0, 1, 2
PIECES = (
    ((Z, X, Y), 3),
    ((Z, Y, X), 3),
    ((X, Y, Z), 2),
    ((Z, X, Y), 3),
    ((Z, Y, X), 3),
    ((Y, X, Z), 2),
)
SCALE_ORDER = (Z, X, Y)
WINDOW = 8


def grid_of(mesh):
    count = mesh.shape["shard"]
    at = [d.coords for d in mesh.devices.reshape(mesh.shape["pair"], count)[0]]
    sizes = tuple(len({c[d] for c in at}) for d in (2, 1, 0))
    return sizes


def power(base, exponent):
    result = jnp.float32(1.0)
    for bit in range(31):
        factor = jnp.float32(base ** (2**bit))
        result = jnp.where((exponent >> bit) & 1 == 1, result * factor, result)
    return result


def kernel(
    grid, limit_ref, step_ref, master_hbm, gradient_hbm, first_hbm, second_hbm,
    new_master, new_first, new_second, codes, scales,
    master, gradient, first, second, mine, my_scales, wide_scales, their_scales,
    plane_sums, line_sums,
    load_sem, plane_send, plane_recv, line_send, line_recv,
    own_send, own_scale_send, peer_send, peer_scale_send, peer_scale_recv,
    pass_send, pass_scale_send, code_recv, scale_recv, local_sem,
):
    sizes = grid
    depth, high, wide = sizes
    plane = high * wide
    half_depth = depth // 2
    sources = half_depth * plane
    height, width = mine.shape
    tiles = width // LANES
    core = lax.axis_index("pair")
    chip = lax.axis_index("shard")
    here = (chip // plane, (chip // wide) % high, chip % wide)
    keeper = here[Z] // half_depth
    peer = 1 - core

    def chip_at(at):
        return (at[Z] * high + at[Y]) * wide + at[X]

    loads = [
        pltpu.make_async_copy(source, held, load_sem.at[i])
        for i, (source, held) in enumerate(
            ((gradient_hbm, gradient), (master_hbm, master), (first_hbm, first), (second_hbm, second))
        )
    ]
    for load in loads:
        load.start()

    barrier = pltpu.get_barrier_semaphore()
    group = 2 * plane
    my_place = core * plane + here[Y] * wide + here[X]

    def greet(device):
        pl.semaphore_signal(barrier, inc=1, device_id=device, device_id_type=MESH)

    for place in range(group):
        @pl.when(place != my_place)
        def _():
            greet((place // plane, here[Z] * plane + place % plane))

    for other in range(depth):
        for side in range(2):
            @pl.when(other != here[Z])
            def _():
                greet((side, chip_at((other, here[Y], here[X]))))

    pl.semaphore_wait(barrier, group - 1 + 2 * (depth - 1))

    loads[0].wait()

    def square(i, total):
        rows = gradient[pl.ds(pl.multiple_of(i * 8, 8), 8), :]
        for j in range(tiles):
            part = rows[:, j * LANES : (j + 1) * LANES]
            total = total + part * part
        return total

    total = lax.fori_loop(0, height // 8, square, jnp.zeros((8, LANES), jnp.float32))

    def exchange(value, buffer, place, count, device_of, send_sem, recv_sem):
        buffer[place] = jnp.sum(value, axis=0, keepdims=True)

        def copy(other, slot, sem):
            return pltpu.make_async_remote_copy(
                src_ref=buffer.at[slot], dst_ref=buffer.at[slot],
                send_sem=send_sem.at[other], recv_sem=recv_sem.at[sem],
                device_id=device_of(other), device_id_type=MESH,
            )

        for other in range(count):
            @pl.when(other != place)
            def _():
                copy(other, place, place).start()

        for other in range(count):
            @pl.when(other != place)
            def _():
                copy(other, place, place).wait_send()
                copy(other, other, other).wait_recv()

        return jnp.sum(buffer[...], axis=0)

    total = exchange(
        total, plane_sums, my_place, group,
        lambda place: (place // plane, here[Z] * plane + place % plane), plane_send, plane_recv,
    )
    total = exchange(
        total, line_sums, here[Z], depth,
        lambda other: (core, chip_at((other, here[Y], here[X]))), line_send, line_recv,
    )
    squares = jnp.sum(total, axis=1, keepdims=True)
    norm_limit = jnp.full((1, 1), limit_ref[0], jnp.float32)
    clip_factor = norm_limit / jnp.maximum(jnp.sqrt(squares), norm_limit)
    one = jnp.ones((1, 1), jnp.float32)
    first_gain = one / (one - power(beta_first, step_ref[0]))
    second_gain = one / (one - power(beta_second, step_ref[0]))
    for load in loads[1:]:
        load.wait()

    def children(source, order):
        last = jnp.int32(-1)
        for i, dim in enumerate(order):
            last = jnp.where(here[dim] != source[dim], i, last)
        ways = []
        for i, dim in enumerate(order):
            for side, step in enumerate((1, -1)):
                if sizes[dim] < 2:
                    continue
                there = list(here)
                there[dim] = here[dim] + step
                inside = (there[dim] >= 0) & (there[dim] < sizes[dim])
                away = (here[dim] - source[dim]) * step > 0
                used = inside & ((last < i) | ((last == i) & away))
                ways.append((used, 2 * dim + side, chip_at(there)))
        return ways

    starts = []
    at = 0
    for order, share in PIECES:
        size = tiles * share // sum(s for _, s in PIECES)
        starts.append((at, size))
        at += size
    assert at == tiles

    def code_slice(source, column, k):
        row = (chip_at(source) % sources) * height
        start, size = starts[k]
        lane = column * width + start * LANES
        return codes.at[
            pl.ds(pl.multiple_of(row, 16), height), pl.ds(pl.multiple_of(lane, LANES), size * LANES)
        ]

    def scale_slice(source):
        row = (chip_at(source) % sources) * height
        return scales.at[pl.ds(pl.multiple_of(row, 16), height), :]

    def my_index():
        return chip % sources

    def own_copy(k, send_sem, to):
        start, size = starts[k]
        return pltpu.make_async_remote_copy(
            src_ref=mine.at[:, pl.ds(start * LANES, size * LANES)],
            dst_ref=code_slice(here, core, k),
            send_sem=send_sem, recv_sem=code_recv.at[my_index(), core, k],
            device_id=(keeper, to), device_id_type=MESH,
        )

    def own_local(k):
        start, size = starts[k]
        return pltpu.make_async_copy(
            mine.at[:, pl.ds(start * LANES, size * LANES)], code_slice(here, core, k), local_sem.at[k]
        )

    lane = lax.broadcasted_iota(jnp.int32, (1, LANES), 1)
    pick_row = lax.broadcasted_iota(jnp.int32, (LANES, LANES), 0)
    pick_column = lax.broadcasted_iota(jnp.int32, (LANES, LANES), 1)
    per_tile = LANES // BLOCK
    step_rows = next(r for r in (64, 48, 32, 16) if height % r == 0)

    def tile(i, carry):
        j, r = i // (height // step_rows), i % (height // step_rows)
        rows = pl.ds(pl.multiple_of(r * step_rows, 16), step_rows)
        where = (rows, pl.ds(pl.multiple_of(j * LANES, LANES), LANES))
        weight = master[where]
        clipped = clip_factor * gradient[where]
        moment = beta_first * first[where] + (1.0 - beta_first) * clipped
        power_moment = beta_second * second[where] + (1.0 - beta_second) * clipped * clipped
        new_first[where] = moment
        new_second[where] = power_moment
        update = moment * first_gain / (jnp.sqrt(power_moment * second_gain) + adam_eps)
        weight = weight - learn_rate * (update + decay_rate * weight)
        new_master[where] = weight
        largest = jnp.abs(weight)
        shift = BLOCK // 2
        while shift:
            ahead = pltpu.roll(largest, LANES - shift, axis=1)
            behind = pltpu.roll(largest, shift, axis=1)
            largest = jnp.maximum(largest, jnp.where((lane & shift) == 0, ahead, behind))
            shift //= 2
        scale = jnp.maximum(largest, scale_floor).astype(jnp.bfloat16)
        mine[where] = (weight / scale.astype(jnp.float32)).astype(jnp.bfloat16)
        target = (core * tiles + j) * per_tile + pick_row // BLOCK
        pick = ((pick_row % BLOCK == 0) & (pick_column == target)).astype(jnp.float32)
        wide_scales[rows, :] += jnp.dot(
            scale, pick.astype(jnp.bfloat16), preferred_element_type=jnp.float32
        )
        return carry

    wide_scales[...] = jnp.zeros_like(wide_scales)
    per = height // step_rows
    for k, (order, _) in enumerate(PIECES):
        start, size = starts[k]
        lax.fori_loop(start * per, (start + size) * per, tile, 0)
        for used, way, to in children(here, order):
            @pl.when(used)
            def _():
                own_copy(k, own_send.at[k, way], to).start()

        @pl.when(core == keeper)
        def _():
            own_local(k).start()

        @pl.when(core != keeper)
        def _():
            own_copy(k, peer_send.at[k], chip).start()

    my_scales[...] = wide_scales[...].astype(jnp.bfloat16)
    peer_scales = pltpu.make_async_remote_copy(
        src_ref=my_scales, dst_ref=their_scales, send_sem=peer_scale_send.at[0],
        recv_sem=peer_scale_recv.at[0], device_id=(peer, chip), device_id_type=MESH,
    )

    def scale_copy(source, send_sem, to):
        index = chip_at(source) % sources
        return pltpu.make_async_remote_copy(
            src_ref=scale_slice(source), dst_ref=scale_slice(source),
            send_sem=send_sem, recv_sem=scale_recv.at[index],
            device_id=(core, to), device_id_type=MESH,
        )

    @pl.when(core != keeper)
    def _():
        peer_scales.start()

    @pl.when(core == keeper)
    def _():
        peer_scales.wait_recv()
        merged = wide_scales[...] + their_scales[...].astype(jnp.float32)
        row = pl.ds(pl.multiple_of(my_index() * height, 16), height)
        scales[row, :] = merged.astype(jnp.bfloat16)
        for used, way, to in children(here, SCALE_ORDER):
            @pl.when(used)
            def _():
                scale_copy(here, own_scale_send.at[way], to).start()

    low = core * half_depth
    top = low + half_depth - 1

    def source_of(q):
        i, j = q // plane, q % plane
        inside = low + (here[Z] - low + i + depth) % half_depth
        z = jnp.where(here[Z] >= top, top - i, jnp.where(here[Z] <= low, low + i, inside))
        return (z, (here[Y] + j // wide) % high, (here[X] + j % wide) % wide)

    def code_copy(source, column, k, send_sem, to):
        index = chip_at(source) % sources
        part = code_slice(source, column, k)
        return pltpu.make_async_remote_copy(
            src_ref=part, dst_ref=part, send_sem=send_sem,
            recv_sem=code_recv.at[index, column, k],
            device_id=(core, to), device_id_type=MESH,
        )

    def drain(q):
        source = source_of(q)
        slot = q % WINDOW

        @pl.when(chip_at(source) != chip)
        def _():
            for k, (order, _) in enumerate(PIECES):
                for column in range(2):
                    for used, way, to in children(source, order):
                        @pl.when(used)
                        def _():
                            code_copy(source, column, k, pass_send.at[slot, column, k, way], to).wait_send()

            for used, way, to in children(source, SCALE_ORDER):
                @pl.when(used)
                def _():
                    scale_copy(source, pass_scale_send.at[slot, way], to).wait_send()

    def forward(q, carry):
        source = source_of(q)
        slot = q % WINDOW
        mine_too = chip_at(source) == chip
        if sources > WINDOW:
            @pl.when(q >= WINDOW)
            def _():
                drain(q - WINDOW)

        @pl.when(mine_too)
        def _():
            for k in range(len(PIECES)):
                own_local(k).wait()
                code_copy(source, peer, k, peer_send.at[k], chip).wait_recv()

        @pl.when(jnp.logical_not(mine_too))
        def _():
            for k, (order, _) in enumerate(PIECES):
                ways = children(source, order)
                for column in range(2):
                    code_copy(source, column, k, peer_send.at[k], chip).wait_recv()
                    for used, way, to in ways:
                        @pl.when(used)
                        def _():
                            code_copy(source, column, k, pass_send.at[slot, column, k, way], to).start()

            scale_copy(source, peer_scale_send.at[0], chip).wait_recv()
            for used, way, to in children(source, SCALE_ORDER):
                @pl.when(used)
                def _():
                    scale_copy(source, pass_scale_send.at[slot, way], to).start()

        return carry

    lax.fori_loop(0, sources, forward, 0)

    def drain_step(q, carry):
        drain(q)
        return carry

    lax.fori_loop(max(0, sources - WINDOW), sources, drain_step, 0)
    for k, (order, _) in enumerate(PIECES):
        for used, way, to in children(here, order):
            @pl.when(used)
            def _():
                own_copy(k, own_send.at[k, way], to).wait_send()

        @pl.when(core != keeper)
        def _():
            own_copy(k, peer_send.at[k], chip).wait_send()

    @pl.when(core != keeper)
    def _():
        peer_scales.wait_send()

    @pl.when(core == keeper)
    def _():
        for used, way, to in children(here, SCALE_ORDER):
            @pl.when(used)
            def _():
                scale_copy(here, own_scale_send.at[way], to).wait_send()


def per_device(grid, master, gradient, first_moment, second_moment, max_norm, step_count):
    height, width = master.shape
    plane = grid[1] * grid[2]
    sources = grid[0] * plane // 2
    pieces = len(PIECES)
    kept = sources * height
    state = jax.ShapeDtypeStruct(master.shape, jnp.float32)
    held = pltpu.VMEM(master.shape, jnp.float32)
    narrow = pltpu.VMEM((height, LANES), jnp.bfloat16)
    dma = pltpu.SemaphoreType.DMA
    vmem = pl.BlockSpec(memory_space=pltpu.VMEM)
    smem = pl.BlockSpec(memory_space=pltpu.SMEM)
    hbm = pl.BlockSpec(memory_space=pl.ANY)
    return pl.pallas_call(
        functools.partial(kernel, grid),
        out_shape=(
            pltpu.VMEM(master.shape, jnp.float32),
            pltpu.VMEM(master.shape, jnp.float32),
            pltpu.VMEM(master.shape, jnp.float32),
            pltpu.VMEM((kept, 2 * width), jnp.bfloat16),
            pltpu.VMEM((kept, 2 * width // BLOCK), jnp.bfloat16),
        ) if VMEM_OUT else (
            state, state, state,
            jax.ShapeDtypeStruct((kept, 2 * width), jnp.bfloat16),
            jax.ShapeDtypeStruct((kept, 2 * width // BLOCK), jnp.bfloat16),
        ),
        in_specs=[smem, smem, hbm, hbm, hbm, hbm],
        out_specs=(vmem,) * 5,
        scratch_shapes=[
            held, held, held, held,
            pltpu.VMEM((height, width), jnp.bfloat16),
            narrow,
            pltpu.VMEM((height, LANES), jnp.float32),
            narrow,
            pltpu.VMEM((2 * plane, 1, LANES), jnp.float32),
            pltpu.VMEM((grid[0], 1, LANES), jnp.float32),
            dma((4,)),
            dma((2 * plane,)), dma((2 * plane,)), dma((grid[0],)), dma((grid[0],)),
            dma((pieces, 6)), dma((6,)), dma((pieces,)), dma((1,)), dma((1,)),
            dma((WINDOW, 2, pieces, 6)), dma((WINDOW, 6)),
            dma((sources, 2, pieces)), dma((sources,)), dma((pieces,)),
        ],
        compiler_params=pltpu.CompilerParams(
            collective_id=0, has_side_effects=True, vmem_limit_bytes=KERNEL_VMEM
        ),
    )(max_norm, step_count, master, gradient, first_moment, second_moment)


VMEM_OUT = False
KERNEL_VMEM = 48 * 1024 * 1024


def solution(mesh):
    return jax.shard_map(
        functools.partial(per_device, grid_of(mesh)),
        mesh=mesh,
        in_specs=(
            P("shard", "pair"),
            P("shard", "pair"),
            P("shard", "pair"),
            P("shard", "pair"),
            P(),
            P(),
        ),
        out_specs=(
            P("shard", "pair"),
            P("shard", "pair"),
            P("shard", "pair"),
            P("pair", None),
            P("pair", None),
        ),
        check_vma=False,
    )
```

time: 291 us -> 145 us (0.50)
  Pallas kernels: 0 us -> 128 us
  blocking collectives: 105 us -> 0 us
  waiting for transfers between devices: 94.9 us -> 0 us
  local copies, waits for them, and re-layouts: 51.7 us -> 14.8 us
  between operations: 16.3 us -> 1.93 us
  starting transfers between devices: 12.2 us -> 0 us
  other arithmetic: 8.64 us -> 0 us
    pallas_call x0 -> x1, Pallas kernels: none -> 128 us  [per_device(): pl.pallas_call(functools.partial(kernel, grid), out_shape=(pltpu.VMEM(mas...]
    all_gather x1 -> x0, waiting for transfers between devices: 94.9 us -> none  [per_device(): lax.all_gather(own_codes, 'shard', axis=0, tiled=True)]
    psum x1 -> x0, blocking collectives: 40.9 us -> none  [per_device(): squares = lax.psum(jnp.sum(gradient * gradient), ('pair', 'shard'))]
    all_gather x1 -> x0, blocking collectives: 38.4 us -> none  [per_device(): lax.all_gather(own_scales, 'shard', axis=0, tiled=True)]
    all_to_all x1 -> x0, blocking collectives: 26 us -> none  [per_device(): lax.all_to_all(half_codes, 'pair', split_axis=0, concat_axis=1, tiled=True)]
    all_to_all x3 -> x0, local copies, waits for them, and re-layouts: 18 us -> none  [the longest x1 16.6 us: per_device(): lax.all_to_all(half_codes, 'pair', split_axis=0, concat_axis=1, tiled=True)]
    unnamed x19 -> x5, local copies, waits for them, and re-layouts: 32.1 us -> 14.8 us
    all_to_all x1 -> x0, starting transfers between devices: 12.2 us -> none  [per_device(): lax.all_to_all(half_scales, 'pair', split_axis=0, concat_axis=1, tiled=True)]
  transfers between devices with their start and end apart: 2 -> 0, of which waited for: 1 -> 0; matrix products, arithmetic and copies ran while one was open for 3% -> 0% of each run, Pallas kernels for 0% -> 0%
where the time goes in v1:
time: 145 us
  Pallas kernels  128 us (88%)
  local copies, waits for them, and re-layouts  14.8 us (10%)
  between operations  1.93 us (1%)
    pallas_call x1, Pallas kernels, per_device(): pl.pallas_call(functools.partial(kernel, grid), out_shape=(pltpu.VMEM(mas...  128 us
    unnamed x5, local copies, waits for them, and re-layouts  14.8 us

profile of v1, /device:TPU:1, one launch (start us, length us, event | category | flops | bytes accessed | tf_op | source)
XLA Modules:
  0.0 145.1 jit_solution(9164199857912919675)
XLA Ops:
  1.9 128.3 %shard_map.101 = (f32[192,2048]{1,0:T(8,128)S(1)}, f32[192,2048]{1,0:T(8,128)S(1)}, f32[192,2048]{1,0:T(8,128)S(1)}, bf16[1536,4096]{1,0:T(8,128)(2,1)}, bf16[1536,128]{1,0:T(8,128)(2,1)S(1)}) custom-call(f32[1]{0:T(128)S(6)} %copy.16.limit_ref, s32[1]{0:T(128)S(6)} %copy.17.step_ref, f32[192,2048]{1,0:T(8,128)} %master_hbm.1, f32[192,2048]{1,0:T(8,128)} %gradient_hbm.1, ...), custom_call_target="tpu_custom_call" | custom-call | tf_op jit(solution)/shard_map/pallas_call | solution.py:403
  130.3 1.1 copy.18
  131.4 1.1 copy.19
  132.6 1.1 copy.20
  133.7 10.6 %copy.21 = bf16[1536,4096]{1,0:T(8,128)(2,1)} copy(bf16[1536,4096]{1,0:T(8,128)(2,1)} %get-tuple-element.13) | data formatting | bytes 25165824
  144.3 0.7 copy.22

commit v2 on v1

--- a/solution.py
+++ b/solution.py
@@ -399,22 +399,21 @@
     dma = pltpu.SemaphoreType.DMA
     vmem = pl.BlockSpec(memory_space=pltpu.VMEM)
     smem = pl.BlockSpec(memory_space=pltpu.SMEM)
-    hbm = pl.BlockSpec(memory_space=pl.ANY)
-    return pl.pallas_call(
+    hbm = pl.BlockSpec(memory_space=pltpu.HBM)
+    free = pl.BlockSpec(memory_space=pl.ANY)
+    state_in = [
+        pltpu.with_memory_space_constraint(a, pltpu.HBM)
+        for a in (master, gradient, first_moment, second_moment)
+    ]
+    results = pl.pallas_call(
         functools.partial(kernel, grid),
         out_shape=(
-            pltpu.VMEM(master.shape, jnp.float32),
-            pltpu.VMEM(master.shape, jnp.float32),
-            pltpu.VMEM(master.shape, jnp.float32),
-            pltpu.VMEM((kept, 2 * width), jnp.bfloat16),
-            pltpu.VMEM((kept, 2 * width // BLOCK), jnp.bfloat16),
-        ) if VMEM_OUT else (
             state, state, state,
             jax.ShapeDtypeStruct((kept, 2 * width), jnp.bfloat16),
             jax.ShapeDtypeStruct((kept, 2 * width // BLOCK), jnp.bfloat16),
         ),
         in_specs=[smem, smem, hbm, hbm, hbm, hbm],
-        out_specs=(vmem,) * 5,
+        out_specs=(vmem, vmem, vmem, free, vmem),
         scratch_shapes=[
             held, held, held, held,
             pltpu.VMEM((height, width), jnp.bfloat16),
@@ -432,11 +431,37 @@
         compiler_params=pltpu.CompilerParams(
             collective_id=0, has_side_effects=True, vmem_limit_bytes=KERNEL_VMEM
         ),
-    )(max_norm, step_count, master, gradient, first_moment, second_moment)
-
-
-VMEM_OUT = False
-KERNEL_VMEM = 48 * 1024 * 1024
+    )(max_norm, step_count, *state_in)
+    return pl.pallas_call(
+        flush,
+        out_shape=tuple(jax.ShapeDtypeStruct(r.shape, r.dtype) for r in results),
+        in_specs=[free] * len(results),
+        out_specs=(hbm,) * len(results),
+        scratch_shapes=[dma((len(results), PARTS))],
+        compiler_params=pltpu.CompilerParams(vmem_limit_bytes=FLUSH_VMEM),
+    )(*results)
+
+
+def flush(*refs):
+    count = len(refs) // 2
+    sem = refs[-1]
+    copies = []
+    for i, (held, out) in enumerate(zip(refs[:count], refs[count:-1])):
+        rows = held.shape[0] // PARTS
+        for part in range(PARTS):
+            span = pl.ds(part * rows, rows)
+            copies.append(pltpu.make_async_copy(held.at[span], out.at[span], sem.at[i, part]))
+    for copy in copies:
+        copy.start()
+    for copy in copies:
+        copy.wait()
+
+
+PARTS = 2
+FLUSH_VMEM = 1024 * 1024
+
+
+KERNEL_VMEM = 16 * 1024 * 1024
 
 
 def solution(mesh):

time: 145 us -> 132 us (0.910)
  local copies, waits for them, and re-layouts: 14.8 us -> 0 us
  Pallas kernels: 128 us -> 130 us
    unnamed x5 -> x0, local copies, waits for them, and re-layouts: 14.8 us -> none
    pallas_call x1 -> x2, Pallas kernels: 128 us -> 130 us  [the longest x1 124 us: per_device(): pl.pallas_call(functools.partial(kernel, grid), out_shape=(state, state,...]
where the time goes in v2:
time: 132 us
  Pallas kernels  130 us (98%)
  between operations  1.93 us (1%)
    pallas_call x1, Pallas kernels, per_device(): pl.pallas_call(functools.partial(kernel, grid), out_shape=(state, state,...  124 us
    pallas_call x1, Pallas kernels, per_device(): pl.pallas_call(flush, out_shape=tuple((jax.ShapeDtypeStruct(r.shape, r.dt...  6.24 us

profile of v2, /device:TPU:1, one launch (start us, length us, event | category | flops | bytes accessed | tf_op | source)
XLA Modules:
  0.0 131.9 jit_solution(14862969422361297502)
XLA Ops:
  1.9 123.8 %shard_map.101 = (f32[192,2048]{1,0:T(8,128)S(1)}, f32[192,2048]{1,0:T(8,128)S(1)}, f32[192,2048]{1,0:T(8,128)S(1)}, bf16[1536,4096]{1,0:T(8,128)(2,1)S(1)}, bf16[1536,128]{1,0:T(8,128)(2,1)S(1)}) custom-call(f32[1]{0:T(128)S(6)} %copy.11.limit_ref, s32[1]{0:T(128)S(6)} %copy.12.step_ref, f32[192,2048]{1,0:T(8,128)} %master_hbm.1, f32[192,2048]{1,0:T(8,128)} %gradient_hbm.1, ...), custom_call_target="tpu_custom_call" | custom-call | tf_op jit(solution)/shard_map/pallas_call | solution.py:408
  125.7 6.2 %shard_map.102 = (f32[192,2048]{1,0:T(8,128)}, f32[192,2048]{1,0:T(8,128)}, f32[192,2048]{1,0:T(8,128)}, bf16[1536,4096]{1,0:T(8,128)(2,1)}, bf16[1536,128]{1,0:T(8,128)(2,1)}) custom-call(f32[192,2048]{1,0:T(8,128)S(1)} %get-tuple-element.10.refs_0_, f32[192,2048]{1,0:T(8,128)S(1)} %get-tuple-element.11.refs_1_, f32[192,2048]{1,0:T(8,128)S(1)} %get-tuple-element.12.refs_2_, ...), custom_call_target="tpu_custom_call" | custom-call | tf_op jit(solution)/shard_map/pallas_call | solution.py:435
